TPU v7x, 32 devices: a whole 2x2x4 slice. The times are simulated.
32 devices in a mesh: row: 4 (over y, core), col: 8 (over z, x).
Axes of the slice: x: 2, y: 2, z: 4, core: 2. Of those that a mesh axis runs over, the one named last changes fastest.
Arguments:
- l_saved: bfloat16 [16, 4, 256, 8, 256], P(None, 'row', None, 'col'), as said below
- l_grad: bfloat16 [16, 4, 256, 8, 256], P(None, 'row', None, 'col'), as said below
Outputs:
- grad_out: float32 [16, 4, 256, 8, 256], P(None, 'row', None, 'col')
Inputs may be any that keep to these rules, and one draw needn't show every extreme that they name: Read as one matrix of 16384 rows, l_saved is lower triangular with its diagonal between 1 and 2. Read as one matrix, l_grad is zero above the diagonal.
All inputs are finite; a program needn't handle non-finite values.
Results may differ from a plain program's by a relative error of at most 0.0003.
Values may be sent and summed in bfloat16 or wider, within the bound.
No kernel may reach another device: no remote copies, remote signals or barrier semaphores. Data moves between devices by JAX's collectives and lax.ppermute only.
A program may use at most 64 MiB of HBM per device.

v0:
```python
import jax
import jax.numpy as jnp
from jax import lax
from jax.sharding import PartitionSpec as P

HIGH = lax.Precision.HIGHEST


def from_root(array, axis, root):
    mine = lax.axis_index(axis) == root
    return lax.psum(jnp.where(mine, array, jnp.zeros_like(array)), axis)


def right_solve(factor, rhs):
    return lax.linalg.triangular_solve(factor, rhs, left_side=False, lower=True)


def diag_gradient(factor, lower_part):
    eye = jnp.eye(factor.shape[0], dtype=jnp.float32)
    middle = jnp.dot(factor.T, lower_part, precision=HIGH, preferred_element_type=jnp.float32)
    middle = jnp.tril(middle) - 0.5 * middle * eye
    half = lax.linalg.triangular_solve(factor, middle, left_side=True, lower=True, transpose_a=True)
    full = right_solve(factor, half)
    return full + full.T


def stacked_inner(left, right):
    flat_left = left.reshape(-1, left.shape[-1])
    flat_right = right.reshape(-1, right.shape[-1]).astype(jnp.float32)
    return lax.dot_general(
        flat_left,
        flat_right,
        (((0,), (0,)), ((), ())),
        precision=HIGH,
        preferred_element_type=jnp.float32,
    )


def solve_rows(diag_factor, column, below):
    rows_here, tile = (column.shape[0], column.shape[1])
    inverse = right_solve(diag_factor, jnp.eye(tile, dtype=jnp.float32))
    solved = jnp.dot(
        column.reshape(-1, tile), inverse, precision=HIGH, preferred_element_type=jnp.float32
    ).reshape(rows_here, tile, tile)
    return jnp.where(below, solved, jnp.float32(0.0))


def diag_down(piece, owner_row):
    return from_root(piece, "row", owner_row).astype(jnp.float32)


def per_device(l_saved, l_grad):
    rows_here = l_saved.shape[0]
    tile = l_saved.shape[2]
    n_row = lax.axis_size("row")
    n_col = lax.axis_size("col")
    factor = l_saved.reshape(rows_here, tile, tile)
    grad = l_grad.reshape(rows_here, tile, tile).astype(jnp.float32)
    my_row = lax.axis_index("row")
    my_col = lax.axis_index("col")
    tile_rows = jnp.arange(rows_here, dtype=jnp.int32) * n_row + my_row
    eye = jnp.eye(tile, dtype=jnp.float32)
    for panel in (n_col - 1, n_col - 2):
        owner_row = panel % n_row
        local = panel // n_row
        at_owner = my_row == owner_row
        below = (tile_rows > panel)[:, None, None]
        diag_factor = diag_down(factor[local], owner_row)
        cbar = solve_rows(diag_factor, grad, below)
        term = jnp.where(at_owner, grad[local], jnp.float32(0.0)) - stacked_inner(cbar, factor)
        total = lax.psum(term, "row")
        sym = diag_gradient(diag_factor, jnp.tril(total))
        sent = from_root(jnp.concatenate([cbar, sym[None]], 0), "col", panel)
        cbar = sent[:rows_here]
        sym = sent[rows_here]
        row_factor = from_root(factor[local], "row", owner_row).astype(jnp.float32)
        update = jnp.dot(
            cbar.reshape(-1, tile), row_factor, precision=HIGH, preferred_element_type=jnp.float32
        )
        partial_sum = stacked_inner(cbar, factor)
        summed = lax.psum(partial_sum, "row")
        own_row = grad[local] - (
            summed + jnp.dot(sym, row_factor, precision=HIGH, preferred_element_type=jnp.float32)
        )
        updated = grad - update.reshape(rows_here, tile, tile)
        updated = updated.at[local].set(jnp.where(at_owner, own_row, updated[local]))
        abar = jnp.tril(sym) - 0.5 * sym * eye
        panel_col = jnp.where(
            below,
            cbar,
            jnp.where((tile_rows == panel)[:, None, None], abar[None], jnp.float32(0.0)),
        )
        grad = jnp.where(my_col < panel, updated, jnp.where(my_col == panel, panel_col, grad))
    return grad.reshape(l_grad.shape)


def solution(mesh):
    in_specs = (P(None, "row", None, "col", None), P(None, "row", None, "col", None))
    out_specs = P(None, "row", None, "col", None)
    return jax.shard_map(
        per_device, mesh=mesh, in_specs=in_specs, out_specs=out_specs, check_vma=False
    )
```

profile of v0, /device:TPU:0, one launch (start us, length us, event | category | flops | bytes accessed | tf_op | source)
XLA Modules:
  0.0 607.6 jit_solution(4179768059537039904)
XLA Ops:
  8.3 4.3 convert_element_type.13
  12.6 32.2 %all-reduce.21.cloned.1.call-done = (bf16[256,256]{1,0:T(8,128)(2,1)}, bf16[256,256]{1,0:T(8,128)(2,1)}) async-done(((bf16[256,256]{1,0:T(8,128)(2,1)}, bf16[256,256]{1,0:T(8,128)(2,1)}), (bf16[256,256]{1,0:T(8,128)(2,1)}, bf16[256,256]{1,0:T(8,128)(2,1)})) %all-reduce.21.cloned.1.call-update) | async-done | bytes 262160 | tf_op jit(solution)/shard_map/psum | solution.py:11
  50.1 19.7 %custom-call.10 = f32[2,128,128]{1,2,0:T(8,128)S(1)} custom-call(f32[2,128,128]{2,1,0:T(8,128)S(1)} %get-tuple-element.71), custom_call_target="InvertDiagBlocksLowerTriangular" | custom-call | tf_op jit(solution)/shard_map/triangular_solve/custom-call.1 | solution.py:15
  74.6 5.8 copy.9
  80.3 5.0 fusion.5
  85.4 4.7 broadcast_select_fusion
  90.2 27.7 %all-reduce.9.cloned.1.call-done = f32[256,256]{1,0:T(8,128)} async-done(((f32[256,256]{1,0:T(8,128)}), f32[256,256]{1,0:T(8,128)}) %all-reduce.9.cloned.1.call-update) | async-done | bytes 262160 | tf_op jit(solution)/shard_map/psum | solution.py:71
  122.8 4.7 maximum_select_fusion
  127.5 13.2 %all-reduce.13.cloned.1.call-start = ((), (), s32[]{:S(2)}) async-start(), calls=%async_computation.2 | async-start | bytes 524288 | tf_op jit(solution)/shard_map/psum | solution.py:81
  144.7 19.7 %custom-call.13 = f32[2,128,128]{1,2,0:T(8,128)S(1)} custom-call(f32[2,128,128]{2,1,0:T(8,128)S(1)} %get-tuple-element.74), custom_call_target="InvertDiagBlocksLowerTriangular" | custom-call | tf_op jit(solution)/shard_map/triangular_solve/custom-call.1 | solution.py:15
  165.3 125.3 %all-reduce.11.cloned.1.call-done = f32[17,256,256]{2,1,0:T(8,128)} async-done(((f32[17,256,256]{2,1,0:T(8,128)}), f32[17,256,256]{2,1,0:T(8,128)}) %all-reduce.11.cloned.1.call-update) | async-done | bytes 4456464 | tf_op jit(solution)/shard_map/psum | solution.py:11
  292.9 4.1 fusion.83
  297.1 4.9 bitcast_subtract_fusion
  305.0 23.4 %all-reduce.13.cloned.1.call-done = f32[256,256]{1,0:T(8,128)} async-done(((f32[256,256]{1,0:T(8,128)}), f32[256,256]{1,0:T(8,128)}) %all-reduce.13.cloned.1.call-update) | async-done | bytes 262160 | tf_op jit(solution)/shard_map/psum | solution.py:81
  330.5 5.1 fusion
  341.3 4.2 convolution_subtract_fusion.1
  345.6 31.5 %all-reduce.15.cloned.1.call-done = f32[256,256]{1,0:T(8,128)} async-done(((f32[256,256]{1,0:T(8,128)}), f32[256,256]{1,0:T(8,128)}) %all-reduce.15.cloned.1.call-update) | async-done | bytes 262160 | tf_op jit(solution)/shard_map/psum | solution.py:71
  380.3 4.7 maximum_select_fusion.1
  385.3 162.9 %all-reduce.17.cloned.1.call-done = f32[17,256,256]{2,1,0:T(8,128)} async-done(((f32[17,256,256]{2,1,0:T(8,128)}), f32[17,256,256]{2,1,0:T(8,128)}) %all-reduce.17.cloned.1.call-update) | async-done | bytes 4456464 | tf_op jit(solution)/shard_map/psum | solution.py:11
  550.4 4.1 fusion.84
  554.6 5.6 convolution_subtract_fusion
  562.3 23.7 %all-reduce.19.cloned.1.call-done = f32[256,256]{1,0:T(8,128)} async-done(((f32[256,256]{1,0:T(8,128)}), f32[256,256]{1,0:T(8,128)}) %all-reduce.19.cloned.1.call-update) | async-done | bytes 262160 | tf_op jit(solution)/shard_map/psum | solution.py:81
  588.1 5.9 select_bitcast_fusion
  594.0 6.3 %copy.7 = f32[16,1,256,1,256]{4,3,2,1,0:T(1,128)} copy(f32[16,1,256,1,256]{4,2,0,3,1:T(8,128)S(1)} %select_bitcast_fusion) | data formatting | bytes 8388608 | tf_op jit(solution)/shard_map/reshape | solution.py:94
  (98 shorter events, 52.5 us)
Async XLA Ops:
  6.5 38.3 %all-reduce.21.cloned.1.call-start = ((), (), s32[]{:S(2)}) async-start(), calls=%async_computation.6 | async-start | bytes 524288 | tf_op jit(solution)/shard_map/psum | solution.py:11
  8.2 109.7 %all-reduce.9.cloned.1.call-start = ((), (), s32[]{:S(2)}) async-start(), calls=%async_computation | async-start | bytes 524288 | tf_op jit(solution)/shard_map/psum | solution.py:71
  8.3 62.4 %copy-start.3 = (bf16[16,1,256,1,256]{4,2,3,1,0:T(8,128)(2,1)S(1)}, bf16[16,1,256,1,256]{4,2,3,1,0:T(8,128)(2,1)}, u32[]{:S(2)}) copy-start(bf16[16,1,256,1,256]{4,2,3,1,0:T(8,128)(2,1)} %param.11) | copy-start | bytes 6291460
  74.6 5.8 copy-start.2
  85.4 205.3 %all-reduce.11.cloned.1.call-start = ((), (), s32[]{:S(2)}) async-start(), calls=%async_computation.1 | async-start | bytes 8912896 | tf_op jit(solution)/shard_map/psum | solution.py:11
  85.4 32.4 %copy-start.7 = (bf16[256,256]{1,0:T(8,128)(2,1)S(1)}, bf16[256,256]{1,0:T(8,128)(2,1)}, u32[]{:S(2)}) copy-start(bf16[256,256]{1,0:T(8,128)(2,1)} %get-tuple-element.93) | copy-start | bytes 393220
  127.5 201.0 %all-reduce.13.cloned.1.call-start = ((), (), s32[]{:S(2)}) async-start(), calls=%async_computation.2 | async-start | bytes 524288 | tf_op jit(solution)/shard_map/psum | solution.py:81
  290.7 2.2 slice-start.3
  297.0 80.1 %all-reduce.15.cloned.1.call-start = ((), (), s32[]{:S(2)}) async-start(), calls=%async_computation.3 | async-start | bytes 524288 | tf_op jit(solution)/shard_map/psum | solution.py:71
  302.0 2.0 copy-start.5
  335.6 3.8 copy-start
  339.4 1.9 copy-start.1
  339.4 37.7 %copy-start.6 = (bf16[256,256]{1,0:T(8,128)(2,1)S(1)}, bf16[256,256]{1,0:T(8,128)(2,1)}, u32[]{:S(2)}) copy-start(bf16[256,256]{1,0:T(8,128)(2,1)} %get-tuple-element.94) | copy-start | bytes 393220
  345.5 202.7 %all-reduce.17.cloned.1.call-start = ((), (), s32[]{:S(2)}) async-start(), calls=%async_computation.4 | async-start | bytes 8912896 | tf_op jit(solution)/shard_map/psum | solution.py:11
  385.1 201.0 %all-reduce.19.cloned.1.call-start = ((), (), s32[]{:S(2)}) async-start(), calls=%async_computation.5 | async-start | bytes 524288 | tf_op jit(solution)/shard_map/psum | solution.py:81
  548.2 2.2 slice-start.2
  550.4 11.8 %slice-start = ((s8[4456448]{0:T(1024)(128)(4,1)}), s8[262144]{0:T(1024)(128)(4,1)S(1)}, s32[]{:S(2)}) async-start(s8[4456448]{0:T(1024)(128)(4,1)} %bitcast.165), calls=%async_computation.7 | async-start | bytes 524288
  554.6 7.7 %slice-start.1 = ((s8[4456448]{0:T(1024)(128)(4,1)}), s8[4194304]{0:T(1024)(128)(4,1)S(1)}, s32[]{:S(2)}) async-start(s8[4456448]{0:T(1024)(128)(4,1)} %bitcast.165), calls=%async_computation.8 | async-start | bytes 8388608
  560.2 2.0 copy-start.4
Sparse Core Ops, SparseCore 0:
  9.7 35.0 all-reduce.20
  85.5 32.3 all-reduce.8
  127.6 163.0 all-reduce.10
  297.1 31.2 all-reduce.12
  345.7 31.3 all-reduce.14
  385.2 163.0 all-reduce.16
  554.7 31.2 all-reduce.18
where the time goes:
time: 616 us; the launch traced here: 608 us
  waiting for transfers between devices  427 us (69%)
  other arithmetic  73.2 us (12%)
  matrix products  47.7 us (8%)
  local copies, waits for them, and re-layouts  31.8 us (5%)
  between operations  14.3 us (2%)
  starting transfers between devices  13.6 us (2%)
    psum x3, waiting for transfers between devices, from_root(): return lax.psum(jnp.where(mine, array, jnp.zeros_like(array)), axis)  320 us
    psum x2, waiting for transfers between devices, per_device(): total = lax.psum(term, 'row')  59.2 us
    psum x2, waiting for transfers between devices, per_device(): summed = lax.psum(partial_sum, 'row')  47.1 us
    another operation x6, other arithmetic, right_solve(): return lax.linalg.triangular_solve(factor, rhs, left_side=False, lower=True)  41.1 us
    dot_general x4, matrix products, stacked_inner(): lax.dot_general(flat_left, flat_right, (((0,), (0,)), ((), ())), precisio...  17.4 us
    psum x2, starting transfers between devices, per_device(): summed = lax.psum(partial_sum, 'row')  13.4 us
  transfers between devices with their start and end apart: 7, of which 7 were waited for; matrix products, arithmetic and copies ran while one was open for 7% of the time, Pallas kernels for 0%

commit v1 on v0

v1 whole, which is shorter than its diff:
```python
import functools

import jax
import jax.numpy as jnp
from jax import lax
from jax.experimental import pallas as pl
from jax.experimental.pallas import tpu as pltpu
from jax.sharding import PartitionSpec as P

F32 = jnp.float32
BF16 = jnp.bfloat16
VMEM = pl.BlockSpec(memory_space=pltpu.VMEM)
SMEM = pl.BlockSpec(memory_space=pltpu.SMEM)


def split(x):
    if x.dtype == BF16:
        return (x,)
    high = x.astype(BF16)
    return (high, (x - high.astype(F32)).astype(BF16))


def product(left, right, left_dim=1, right_dim=0):
    total = None
    for i, a in enumerate(split(left)):
        for j, b in enumerate(split(right)):
            if i + j < 2:
                term = lax.dot_general(
                    a, b, (((left_dim,), (right_dim,)), ((), ())), preferred_element_type=F32
                )
                total = term if total is None else total + term
    return total


def indices(tile):
    rows = lax.broadcasted_iota(jnp.int32, (tile, tile), 0)
    cols = lax.broadcasted_iota(jnp.int32, (tile, tile), 1)
    return rows, cols


def inverses(factors):
    tile = factors[0].shape[0]
    rows, cols = indices(tile)
    eye = rows == cols
    wide = [f.astype(F32) for f in factors]
    done = [jnp.where(eye, 1.0 / jnp.where(eye, f, 1.0), 0.0) for f in wide]
    size = 1
    while size < tile:
        pair = (rows // (2 * size) == cols // (2 * size)) & (rows // size != cols // size)
        parts = [jnp.where(pair, f, 0.0).astype(BF16) for f in wide]
        steps = [product(w, b) for w, b in zip(done, parts)]
        done = [w - product(s, w) for w, s in zip(done, steps)]
        size *= 2
    return done


def weights_kernel(place, l77, l76, l66, l7, l6, w7_ref, w6_ref, v_ref, high_ref, low_ref):
    tile = l77.shape[0]
    rows, cols = indices(tile)
    minus_eye = jnp.where(rows == cols, -1.0, 0.0)
    w7, w6 = inverses([l77[...], l66[...]])
    last, second = place[0] == 1, place[1] == 1
    row7 = jnp.where(last, minus_eye, jnp.where(second, 0.0, l7[...].astype(F32)))
    row6 = jnp.where(second, minus_eye, jnp.where(last, 0.0, l6[...].astype(F32)))
    x = product(w6, row6.astype(BF16))
    y = product(w7, row7 - product(l76[...], x))
    w7_ref[...] = w7
    w6_ref[...] = w6
    v_ref[...] = product(w7, l76[...])
    for k, value in enumerate((-y, -x)):
        high, low = split(value)
        high_ref[k * tile : (k + 1) * tile, :] = high
        low_ref[k * tile : (k + 1) * tile, :] = low


def weights(place, *tiles):
    tile = tiles[0].shape[0]
    square = jax.ShapeDtypeStruct((tile, tile), F32)
    tall = jax.ShapeDtypeStruct((2 * tile, tile), BF16)
    return pl.pallas_call(
        weights_kernel,
        out_shape=(square, square, square, tall, tall),
        in_specs=[SMEM] + [VMEM] * 5,
        out_specs=(VMEM,) * 5,
        cost_estimate=pl.CostEstimate(flops=120 * tile**3, bytes_accessed=8 * tile**2, transcendentals=0),
        name="weights",
    )(place, *tiles)


def gram_kernel(first, g7, g6, low, w7, w6, v, p_ref):
    tile = w7.shape[0]
    n = g7.shape[0]
    a7 = product(g7[...], low[first:, :], 0, 0)
    a6 = product(g6[...], low[first:, :], 0, 0)
    p_ref[:tile, :] = product(w7[...], a7, 0, 0)
    p_ref[tile:, :] = product(w6[...], a6 - product(v[...], a7, 0, 0), 0, 0)


def grams(first, g7, g6, low, w7, w6, v):
    tile = w7.shape[0]
    return pl.pallas_call(
        functools.partial(gram_kernel, first),
        out_shape=jax.ShapeDtypeStruct((2 * tile, tile), F32),
        in_specs=[VMEM] * 6,
        out_specs=VMEM,
        name="grams",
    )(g7, g6, low, w7, w6, v)


def symmetric(factor, inverse, lower):
    rows, cols = indices(factor.shape[0])
    middle = product(factor, lower, 0, 0)
    phi = jnp.where(rows > cols, middle, jnp.where(rows == cols, 0.5 * middle, 0.0))
    full = product(product(inverse, phi, 0, 0), inverse)
    return full + full.T


def halved(sym):
    rows, cols = indices(sym.shape[0])
    return jnp.where(rows > cols, sym, jnp.where(rows == cols, 0.5 * sym, 0.0))


def tail_kernel(place, t77, t76, t66, l77, l76, l66, w7, w6, l7, l6, g, p, out_ref):
    tile = g.shape[0]
    rows, cols = indices(tile)
    lower = rows >= cols
    last, second, top, bottom = (place[k] == 1 for k in range(4))
    s7 = symmetric(l77[...], w7[...], jnp.where(lower, t77[...], 0.0))
    c67 = product(t76[...] - product(s7, l76[...]), w6[...])
    q6 = jnp.where(lower, t66[...] - product(c67, l76[...], 0, 0), 0.0)
    s6 = symmetric(l66[...], w6[...], q6)
    from7 = jnp.where(top, s7, c67.T)
    from6 = jnp.where(top, c67, s6)
    panel = top | bottom
    gradient = g[...].astype(F32)
    part = jnp.where(top, p[:tile, :], p[tile:, :])
    fresh = gradient - part - product(from7, l7[...]) - product(from6, l6[...])
    left = jnp.where(panel, fresh, gradient)
    at6 = jnp.where(top, c67, jnp.where(bottom, halved(s6), 0.0))
    at7 = jnp.where(top, halved(s7), 0.0)
    out_ref[...] = jnp.where(last, at7, jnp.where(second, at6, left))


def tail(place, *arrays):
    tile = arrays[0].shape[0]
    return pl.pallas_call(
        tail_kernel,
        out_shape=jax.ShapeDtypeStruct((tile, tile), F32),
        in_specs=[SMEM] + [VMEM] * len(arrays),
        out_specs=VMEM,
        name="tail",
    )(place, *arrays)


def out_kernel(first, place, g, g7, g6, high, low, out_ref):
    tile = high.shape[1]
    half = tile // 2
    inside = place[4] == 1

    def put(row, value):
        out_ref[pl.ds(2 * row, tile, stride=2), :] = value[:, :half]
        out_ref[pl.ds(2 * row + 1, tile, stride=2), :] = value[:, half:]

    for t in range(first):
        row = t * tile
        put(row, jnp.where(inside, g[row : row + tile, :].astype(F32), 0.0))

    def step(t, carry):
        row = pl.multiple_of(t * tile, tile)
        total = jnp.where(inside, g[pl.ds(first * tile + row, tile), :].astype(F32), 0.0)
        for k, part in enumerate((g7, g6)):
            block = part[pl.ds(row, tile), :]
            for weight in (high, low):
                total += jnp.dot(
                    block, weight[k * tile : (k + 1) * tile, :], preferred_element_type=F32
                )
        put(first * tile + row, total)
        return carry

    lax.fori_loop(0, g7.shape[0] // tile, step, 0)


def outputs(first, place, g, g7, g6, high, low):
    n, tile = g.shape
    return pl.pallas_call(
        functools.partial(out_kernel, first),
        out_shape=jax.ShapeDtypeStruct((2 * n, tile // 2), F32),
        in_specs=[SMEM] + [VMEM] * 5,
        out_specs=VMEM,
        name="outputs",
    )(place, g, g7, g6, high, low)


def place_kernel(row, tile_ref, whole_ref, out_ref, stage, sem):
    n, tile = tile_ref.shape
    half = tile // 2
    stage[pl.ds(0, n, stride=2), :] = tile_ref[:, :half]
    stage[pl.ds(1, n, stride=2), :] = tile_ref[:, half:]
    copy = pltpu.make_async_copy(stage, out_ref.at[pl.ds(2 * row, 2 * n), :], sem)
    copy.start()
    copy.wait()


def place_tile(row, tile_value, whole):
    n, tile = tile_value.shape
    anywhere = pl.BlockSpec(memory_space=pl.ANY)
    return pl.pallas_call(
        functools.partial(place_kernel, row),
        out_shape=jax.ShapeDtypeStruct(whole.shape, F32),
        in_specs=[VMEM, anywhere],
        out_specs=anywhere,
        scratch_shapes=[pltpu.VMEM((2 * n, tile // 2), F32), pltpu.SemaphoreType.DMA],
        input_output_aliases={1: 0},
        name="place_tile",
    )(tile_value, whole)


def per_device(l_saved, l_grad):
    rows_here, tile = l_saved.shape[0], l_saved.shape[2]
    n_row, n_col = lax.axis_size("row"), lax.axis_size("col")
    if n_col % n_row or n_col % 2 or n_row & (n_row - 1) or n_row < 2:
        raise ValueError("mesh shape")
    first = n_col // n_row
    seven, six = n_col - 1, n_col - 2
    top_row, bottom_row = n_row - 1, n_row - 2
    my_row, my_col = lax.axis_index("row"), lax.axis_index("col")
    hop = (seven - my_col) // 2
    odd = my_col % 2 == seven % 2
    low = l_saved.reshape(rows_here * tile, tile)
    grad = l_grad.reshape(rows_here * tile, tile)
    last, second = my_col == seven, my_col == six
    top, bottom = my_row == top_row, my_row == bottom_row
    place = jnp.stack([last, second, top, bottom, my_col < six]).astype(jnp.int32)

    def down(x):
        reach = 1
        while reach < n_col // 2:
            pairs = [
                (c, c - 2 * reach)
                for c in range(n_col)
                if (seven - c) // 2 < reach and c >= 2 * reach
            ]
            y = lax.ppermute(x, "col", pairs)
            x = jnp.where((hop >= reach) & (hop < 2 * reach), y, x)
            reach *= 2
        return x

    def swap(x):
        return lax.ppermute(x, "col", [(c, c ^ 1) for c in range(n_col)])

    def both(x):
        other = swap(x)
        return jnp.where(odd, x, other), jnp.where(odd, other, x)

    def row_sum(x):
        reach = 1
        while reach < n_row:
            x = x + lax.ppermute(x, "row", [(r, r ^ reach) for r in range(n_row)])
            reach *= 2
        return x

    edge = (first - 1) * tile
    row_tiles = lax.all_gather(low[edge : edge + tile], "row")
    l7, l6 = row_tiles[top_row], row_tiles[bottom_row]
    at7, at6 = both(down(jnp.concatenate([l7, l6], 0)))
    l77, l76, l66 = at7[:tile], at6[:tile], at6[tile:]
    w7, w6, v, high, lowp = weights(place, l77, l76, l66, l7, l6)

    g7, g6 = both(down(grad[first * tile :]))
    part = grams(first * tile, g7, g6, low, w7, w6, v)
    g_tile = grad[edge : edge + tile]
    mine = jnp.where(top & last, g_tile, jnp.zeros_like(g_tile)).astype(F32)
    upper = jnp.where(top & second, g_tile, jnp.zeros_like(g_tile)).astype(F32)
    under = jnp.where(bottom & second, g_tile, jnp.zeros_like(g_tile)).astype(F32)
    tiles = jnp.where(last, jnp.concatenate([mine, under], 0), jnp.concatenate([upper, under], 0)) - part
    total = row_sum(jnp.concatenate([tiles, part], 0))
    s7, s6 = both(down(total[: 2 * tile]))
    t77, t76, t66 = s7[:tile], s6[:tile], s6[tile:]
    tile_out = tail(place, t77, t76, t66, l77, l76, l66, w7, w6, l7, l6, g_tile, total[2 * tile :])
    whole = outputs(first, place, grad, g7, g6, high, lowp)
    whole = place_tile(edge, tile_out, whole)
    return whole.reshape(l_grad.shape)


def solution(mesh):
    spec = P(None, "row", None, "col", None)
    return jax.shard_map(
        per_device, mesh=mesh, in_specs=(spec, spec), out_specs=spec, check_vma=False
    )
```

time: 616 us -> 291 us (0.47); the launches traced: 608 us -> 291 us
  waiting for transfers between devices: 427 us -> 225 us
  other arithmetic: 73.2 us -> 12.6 us
  matrix products: 47.7 us -> 0 us
  Pallas kernels: 0 us -> 28.1 us
  local copies, waits for them, and re-layouts: 31.8 us -> 4.09 us
  between operations: 14.3 us -> 0.19 us
  blocking collectives: 0 us -> 8.68 us
    psum x7 -> x0, waiting for transfers between devices: 427 us -> none  [the longest x3 320 us: from_root(): return lax.psum(jnp.where(mine, array, jnp.zeros_like(array)), axis)]
    ppermute x0 -> x11, waiting for transfers between devices: none -> 225 us  [the longest x6 164 us: down(): y = lax.ppermute(x, 'col', pairs)]
    dot_general x12 -> x0, matrix products: 42.2 us -> none  [the longest x4 17.4 us: stacked_inner(): lax.dot_general(flat_left, flat_right, (((0,), (0,)), ((), ())), precisio...]
    another operation x6 -> x0, other arithmetic: 41.1 us -> none  [right_solve(): return lax.linalg.triangular_solve(factor, rhs, left_side=False, lower=True)]
    pallas_call x0 -> x5, Pallas kernels: none -> 28.1 us  [the longest x1 9.1 us: outputs(): pl.pallas_call(functools.partial(out_kernel, first), out_shape=jax.ShapeD...]
    psum x7 -> x0, starting transfers between devices: 13.6 us -> none  [the longest x2 13.4 us: per_device(): summed = lax.psum(partial_sum, 'row')]
    select_n x5 -> x9, other arithmetic: 20.8 us -> 7.75 us  [the longest x4 4.35 us: both(): return (jnp.where(odd, x, other), jnp.where(odd, other, x))]
    ppermute x0 -> x11, starting transfers between devices: none -> 12.5 us  [the longest x6 7.17 us: down(): y = lax.ppermute(x, 'col', pairs)]
  transfers between devices with their start and end apart: 7 -> 11, of which waited for: 7 -> 7; matrix products, arithmetic and copies ran while one was open for 7% -> 2% of each run, Pallas kernels for 0% -> 5%
where the time goes in v1:
time: 291 us
  waiting for transfers between devices  225 us (77%)
  Pallas kernels  28.1 us (10%)
  other arithmetic  12.6 us (4%)
  starting transfers between devices  12.5 us (4%)
  blocking collectives  8.68 us (3%)
  local copies, waits for them, and re-layouts  4.09 us (1%)
    ppermute x6, waiting for transfers between devices, down(): y = lax.ppermute(x, 'col', pairs)  164 us
    ppermute x3, waiting for transfers between devices, swap(): return lax.ppermute(x, 'col', [(c, c ^ 1) for c in range(n_col)])  34.7 us
    ppermute x2, waiting for transfers between devices, row_sum(): x = x + lax.ppermute(x, 'row', [(r, r ^ reach) for r in range(n_row)])  26.3 us
    pallas_call x1, Pallas kernels, outputs(): pl.pallas_call(functools.partial(out_kernel, first), out_shape=jax.ShapeD...  9.1 us
    all_gather x1, blocking collectives, per_device(): row_tiles = lax.all_gather(low[edge:edge + tile], 'row')  8.68 us
    ppermute x6, starting transfers between devices, down(): y = lax.ppermute(x, 'col', pairs)  7.17 us
    pallas_call x1, Pallas kernels, weights(): pl.pallas_call(weights_kernel, out_shape=(square, square, square, tall, t...  6.58 us
  transfers between devices with their start and end apart: 11, of which 7 were waited for; matrix products, arithmetic and copies ran while one was open for 2% of the time, Pallas kernels for 5%

profile of v1, /device:TPU:0, one launch (start us, length us, event | category | flops | bytes accessed | tf_op | source)
XLA Modules:
  0.0 290.8 jit_solution(16043130254731589312)
XLA Ops:
  0.0 1.6 slice.48
  1.6 1.9 collective-permute-start
  3.6 1.5 broadcast_select_fusion
  5.1 1.3 collective-permute-start.1
  6.4 8.7 %all-gather = bf16[4,1,256,1,256]{4,2,3,1,0:T(8,128)(2,1)S(1)} all-gather(bf16[1,1,256,1,256]{4,2,3,1,0:T(8,128)(2,1)S(1)} %slice-done), channel_id=2, replica_groups=mesh['row'=4,'col'=8] {'row'}, dimensions={0}, use_global_device_ids=true | all-gather | bytes 655360 | tf_op jit(solution)/shard_map/all_gather | solution.py:263
  15.9 119.7 %collective-permute-done.1 = bf16[3584,256]{1,0:T(8,128)(2,1)} collective-permute-done((bf16[3584,256]{1,0:T(8,128)(2,1)}, bf16[3584,256]{1,0:T(8,128)(2,1)}, u32[]{:S(2)}, u32[]{:S(2)}) %collective-permute-start.1) | collective-permute-done | bytes 1835040 | tf_op jit(solution)/shard_map/ppermute | solution.py:243
  135.5 1.7 broadcast_select_fusion.1
  137.2 1.6 collective-permute-start.2
  138.9 1.3 collective-permute-start.4
  140.2 9.4 %collective-permute-done.4 = bf16[512,256]{1,0:T(8,128)(2,1)S(1)} collective-permute-done((bf16[512,256]{1,0:T(8,128)(2,1)S(1)}, bf16[512,256]{1,0:T(8,128)(2,1)S(1)}, u32[]{:S(2)}, u32[]{:S(2)}) %collective-permute-start.4) | collective-permute-done | bytes 262176 | tf_op jit(solution)/shard_map/ppermute | solution.py:243
  151.9 33.0 %collective-permute-done.5 = bf16[512,256]{1,0:T(8,128)(2,1)S(1)} collective-permute-done((bf16[512,256]{1,0:T(8,128)(2,1)S(1)}, bf16[512,256]{1,0:T(8,128)(2,1)S(1)}, u32[]{:S(2)}, u32[]{:S(2)}) %collective-permute-start.5) | collective-permute-done | bytes 262176 | tf_op jit(solution)/shard_map/ppermute | solution.py:249
  186.3 6.6 %weights.1 = (f32[256,256]{1,0:T(8,128)}, f32[256,256]{1,0:T(8,128)}, f32[256,256]{1,0:T(8,128)}, bf16[512,256]{1,0:T(8,128)(2,1)}, bf16[512,256]{1,0:T(8,128)(2,1)}) custom-call(s32[5]{0:T(128)} %convert_element_type.12.place, bf16[256,256]{1,0:T(8,128)(2,1)} %slice_select_fusion.1.l77, bf16[256,256]{1,0:T(8,128)(2,1)} %get-tuple-element.27.l76, ...), custom_call_target="tpu_custom_call" | custom-call | flops 2013265920 | bytes 524288 | tf_op jit(solution)/shard_map/weights/pallas_call | solution.py:80
  192.8 3.6 %broadcast_select_fusion.2 = (bf16[3584,256]{1,0:T(8,128)(2,1)}, bf16[3584,256]{1,0:T(8,128)(2,1)}) fusion(bf16[3584,256]{1,0:T(8,128)(2,1)} %collective-permute-done.2, bf16[3584,256]{1,0:T(8,128)(2,1)S(1)} %broadcast_select_fusion.1, pred[]{:T(512)S(6)} %eq.21), kind=kLoop, calls=%fused_computation.2 | loop fusion | flops 1835008 | bytes 7340033 | tf_op jit(solution)/shard_map/jit(_where)/select_n | solution.py:253
  196.4 5.4 %grams.1 = f32[512,256]{1,0:T(8,128)} custom-call(bf16[3584,256]{1,0:T(8,128)(2,1)} %get-tuple-element.16.g7, bf16[3584,256]{1,0:T(8,128)(2,1)} %get-tuple-element.15.g6, bf16[4096,256]{1,0:T(8,128)(2,1)} %bitcast.24, f32[256,256]{1,0:T(8,128)} %get-tuple-element.10.w7, f32[256,256]{1,0:T(8,128)} %get-tuple-element.11.w6, f32[256,256]{1,0:T(8,128)} %get-tuple-element.12.v), custom_call_target="tpu_custom_call" | custom-call | tf_op jit(solution)/shard_map/grams/pallas_call | solution.py:101
  203.2 2.6 collective-permute-done.6
  206.0 1.6 collective-permute-start.7
  207.5 23.7 %collective-permute-done.7 = f32[1024,256]{1,0:T(8,128)S(1)} collective-permute-done((f32[1024,256]{1,0:T(8,128)S(1)}, f32[1024,256]{1,0:T(8,128)S(1)}, u32[]{:S(2)}, u32[]{:S(2)}) %collective-permute-start.7) | collective-permute-done | bytes 1048608 | tf_op jit(solution)/shard_map/ppermute | solution.py:258
  234.3 34.5 %collective-permute-done.9 = f32[512,256]{1,0:T(8,128)S(1)} collective-permute-done((f32[512,256]{1,0:T(8,128)S(1)}, f32[512,256]{1,0:T(8,128)S(1)}, u32[]{:S(2)}, u32[]{:S(2)}) %collective-permute-start.9) | collective-permute-done | bytes 524320 | tf_op jit(solution)/shard_map/ppermute | solution.py:243
  268.9 1.6 collective-permute-start.10
  270.5 1.6 slice_bitcast_fusion.2.g
  272.1 9.1 %outputs.1.whole_ref = f32[8192,128]{1,0:T(8,128)} custom-call(s32[5]{0:T(128)} %convert_element_type.12.place, bf16[4096,256]{1,0:T(8,128)(2,1)} %bitcast.22, bf16[3584,256]{1,0:T(8,128)(2,1)} %get-tuple-element.16.g7, bf16[3584,256]{1,0:T(8,128)(2,1)} %get-tuple-element.15.g6, bf16[512,256]{1,0:T(8,128)(2,1)} %get-tuple-element.13.high, ...), custom_call_target="tpu_custom_call" | custom-call | tf_op jit(solution)/shard_map/outputs/pallas_call | solution.py:185
  281.2 1.7 collective-permute-done.10
  283.8 5.3 %tail.1.tile_ref = f32[256,256]{1,0:T(8,128)} custom-call(s32[5]{0:T(128)} %convert_element_type.12.place, f32[256,256]{1,0:T(8,128)} %get-tuple-element.28.t77, f32[256,256]{1,0:T(8,128)} %get-tuple-element.23.t76, f32[256,256]{1,0:T(8,128)} %get-tuple-element.22.t66, bf16[256,256]{1,0:T(8,128)(2,1)} %slice_select_fusion.1.l77, ...), custom_call_target="tpu_custom_call" | custom-call | tf_op jit(solution)/shard_map/tail/pallas_call | solution.py:146
  289.2 1.7 place_tile.1
  (36 shorter events, 10.0 us)
Async XLA Ops:
  1.6 2.0 collective-permute-start
  3.6 2.8 slice-start
  5.1 130.4 %collective-permute-start.1 = (bf16[3584,256]{1,0:T(8,128)(2,1)}, bf16[3584,256]{1,0:T(8,128)(2,1)}, u32[]{:S(2)}, u32[]{:S(2)}) collective-permute-start(bf16[3584,256]{1,0:T(8,128)(2,1)} %broadcast_select_fusion), channel_id=1, source_target_pairs={{4,0},{5,1},{6,2},{7,3},{12,8},{13,9},{14,10},{15,11},{20,16},{21,... | collective-permute-start | bytes 5505032 | tf_op jit(solution)/shard_map/ppermute | solution.py:243
  15.1 123.7 %copy-start.1 = (bf16[256,256]{1,0:T(8,128)(2,1)}, bf16[256,256]{1,0:T(8,128)(2,1)S(1)}, u32[]{:S(2)}) copy-start(bf16[256,256]{1,0:T(8,128)(2,1)S(1)} %get-tuple-element.24.l7) | copy-start | bytes 393220
  15.1 123.7 %copy-start.2 = (bf16[256,256]{1,0:T(8,128)(2,1)}, bf16[256,256]{1,0:T(8,128)(2,1)S(1)}, u32[]{:S(2)}) copy-start(bf16[256,256]{1,0:T(8,128)(2,1)S(1)} %get-tuple-element.25.l6) | copy-start | bytes 393220
  15.2 123.6 %collective-permute-start.3 = (bf16[512,256]{1,0:T(8,128)(2,1)S(1)}, bf16[512,256]{1,0:T(8,128)(2,1)S(1)}, u32[]{:S(2)}, u32[]{:S(2)}) collective-permute-start(bf16[512,256]{1,0:T(8,128)(2,1)S(1)} %pad_maximum_fusion.3), channel_id=1, source_target_pairs={{6,4},{7,5},{14,12},{15,13},{22,20},{23,21},{30,28},{31,29}} | collective-permute-start | bytes 786440 | tf_op jit(solution)/shard_map/ppermute | solution.py:243
  137.2 55.6 %collective-permute-start.2 = (bf16[3584,256]{1,0:T(8,128)(2,1)S(1)}, bf16[3584,256]{1,0:T(8,128)(2,1)}, u32[]{:S(2)}, u32[]{:S(2)}) collective-permute-start(bf16[3584,256]{1,0:T(8,128)(2,1)S(1)} %broadcast_select_fusion.1), channel_id=1, source_target_pairs={{0,1},{1,0},{2,3},{3,2},{4,5},{5,4},{6,7},{7,6},{8,9},{9,8},{10,11... | collective-permute-start | bytes 5505032 | tf_op jit(solution)/shard_map/ppermute | solution.py:249
  138.9 10.7 %collective-permute-start.4 = (bf16[512,256]{1,0:T(8,128)(2,1)S(1)}, bf16[512,256]{1,0:T(8,128)(2,1)S(1)}, u32[]{:S(2)}, u32[]{:S(2)}) collective-permute-start(bf16[512,256]{1,0:T(8,128)(2,1)S(1)} %broadcast_select_fusion.5), channel_id=1, source_target_pairs={{4,0},{5,1},{6,2},{7,3},{12,8},{13,9},{14,10},{15,11},{20,16},{21,... | collective-permute-start | bytes 786440 | tf_op jit(solution)/shard_map/ppermute | solution.py:243
  149.6 35.2 %collective-permute-start.5 = (bf16[512,256]{1,0:T(8,128)(2,1)S(1)}, bf16[512,256]{1,0:T(8,128)(2,1)S(1)}, u32[]{:S(2)}, u32[]{:S(2)}) collective-permute-start(bf16[512,256]{1,0:T(8,128)(2,1)S(1)} %broadcast_select_fusion.7), channel_id=1, source_target_pairs={{0,1},{1,0},{2,3},{3,2},{4,5},{5,4},{6,7},{7,6},{8,9},{9,8},{10,11... | collective-permute-start | bytes 786440 | tf_op jit(solution)/shard_map/ppermute | solution.py:249
  201.8 1.2 copy-start
  203.1 2.7 collective-permute-start.6
  206.0 25.3 %collective-permute-start.7 = (f32[1024,256]{1,0:T(8,128)S(1)}, f32[1024,256]{1,0:T(8,128)S(1)}, u32[]{:S(2)}, u32[]{:S(2)}) collective-permute-start(f32[1024,256]{1,0:T(8,128)S(1)} %fusion.2), channel_id=1, source_target_pairs={{0,16},{8,24},{16,0},{24,8},{1,17},{9,25},{17,1},{25,9},{2,18},{10... | collective-permute-start | bytes 3145736 | tf_op jit(solution)/shard_map/ppermute | solution.py:258
  231.4 0.7 collective-permute-start.8
  233.0 35.8 %collective-permute-start.9 = (f32[512,256]{1,0:T(8,128)S(1)}, f32[512,256]{1,0:T(8,128)S(1)}, u32[]{:S(2)}, u32[]{:S(2)}) collective-permute-start(f32[512,256]{1,0:T(8,128)S(1)} %get-tuple-element.21), channel_id=1, source_target_pairs={{4,0},{5,1},{6,2},{7,3},{12,8},{13,9},{14,10},{15,11},{20,16},{21,... | collective-permute-start | bytes 1572872 | tf_op jit(solution)/shard_map/ppermute | solution.py:243
  268.9 13.9 %collective-permute-start.10 = (f32[512,256]{1,0:T(8,128)S(1)}, f32[512,256]{1,0:T(8,128)S(1)}, u32[]{:S(2)}, u32[]{:S(2)}) collective-permute-start(f32[512,256]{1,0:T(8,128)S(1)} %broadcast_select_fusion.6), channel_id=1, source_target_pairs={{0,1},{1,0},{2,3},{3,2},{4,5},{5,4},{6,7},{7,6},{8,9},{9,8},{10,11... | collective-permute-start | bytes 1572872 | tf_op jit(solution)/shard_map/ppermute | solution.py:249
